TPU v7x, 256 devices: a whole 4x4x8 slice. The times are simulated.
256 devices in a mesh: section: 8 (over z), col: 32 (over y, x, core).
Axes of the slice: x: 4, y: 4, z: 8, core: 2. Of those that a mesh axis runs over, the one named last changes fastest.
Arguments:
- tiles: bfloat16 [1024, 12, 128, 128], P('col', None, 'section'), may hold values from 0.0099487305 to 1
- offsets: int32 [1024, 12], replicated, may hold values from -6 to 6, as said below
- counts: int32 [1024], replicated, may hold values from 1 to 12
- ranks: int32 [1024, 25, 128, 128], P('col', None, 'section'), may hold values from 0 to 3199, as said below
Outputs:
- pruned: bfloat16 [1024, 25, 128, 128], P('col', None, 'section')
Inputs may be any that keep to these rules, and one draw needn't show every extreme that they name: Within each panel the 12 offsets are distinct, each from -6 to 6. For every panel j and column c, ranks[j, :, c, :] holds each of 0 .. 3199 once.
All inputs are finite; a program needn't handle non-finite values.
Results may differ from a plain program's by a relative error of at most 0.001.
Values may be sent and summed in bfloat16 or wider, within the bound.
A program may use at most 128 MiB of HBM per device.

v0:
```python
import jax
import jax.numpy as jnp
from jax import lax
from jax.sharding import PartitionSpec as P

W = 6
TOPK = 256


def extended(shard, sides, width):
    for axis, dim in sides:
        count, length = (lax.axis_size(axis), shard.shape[dim])
        up = [(i, (i + 1) % count) for i in range(count - 1)]
        down = [(j, i) for i, j in up]
        last = lax.slice_in_dim(shard, length - width, length, axis=dim)
        initial = lax.slice_in_dim(shard, 0, width, axis=dim)
        before = lax.ppermute(last, axis, up)
        after = lax.ppermute(initial, axis, down)
        shard = jnp.concatenate([before, shard, after], axis=dim)
    return shard


def cut_along(shard, dim, count):
    before, after = (shard.shape[:dim], shard.shape[dim + 1 :])
    return jnp.moveaxis(shard.reshape(*before, count, -1, *after), dim, 0)


def piece_ends(length, count):
    unit = 8 if length >= 8 * count else 1
    return [length // unit * k // count * unit for k in range(1, count)]


def joined_along(tiles, dim):
    tiles = jnp.moveaxis(tiles, 0, dim)
    dims = tiles.shape
    return tiles.reshape(*dims[:dim], dims[dim] * dims[dim + 1], *dims[dim + 2 :])


def exchange_in_pieces(shard, axis, pieces, split_dim, concat_dim):
    tiles = cut_along(shard, split_dim, lax.axis_size(axis))
    split_at = max(range(1, max(2, tiles.ndim - 1)), key=lambda d: tiles.shape[d])
    outs = []
    for share in jnp.split(tiles, piece_ends(tiles.shape[split_at], pieces), axis=split_at):
        if share.size:
            outs.append(lax.all_to_all(share, axis, split_axis=0, concat_axis=0, tiled=True))
    return joined_along(jnp.concatenate(outs, axis=split_at), concat_dim)


def expand(own, own_off, own_cnt, center, global_panel, banded, band_off, band_cnt, total, bands):
    slots = own.shape[0]
    slot_ids = jnp.arange(slots, dtype=jnp.int32)
    where_at = center + W + own_off
    firsts = banded[where_at]
    first_off = band_off[where_at]
    first_cnt = band_cnt[where_at]
    row_own = global_panel + own_off
    ok_own = (slot_ids < own_cnt) & (row_own >= 0) & (row_own < total)
    row_first = row_own[:, None] + first_off
    ok_first = (slot_ids[None, :] < first_cnt[:, None]) & (row_first >= 0) & (row_first < total)
    weight = (ok_own[:, None] & ok_first).astype(jnp.float32)
    target = own_off[:, None] + first_off + 2 * W
    products = jnp.einsum("kcx,klxr->klcr", own, firsts, preferred_element_type=jnp.float32)
    weighted = products * weight[:, :, None, None]
    columns = own.shape[1]
    rows = own.shape[2]
    empty = jnp.zeros((bands, columns, rows), jnp.float32)
    return empty.at[target.reshape(-1)].add(weighted.reshape((slots * slots, columns, rows)))


def finish(expanded, rank_block):
    keep = rank_block < TOPK
    squared = jnp.where(keep, expanded * expanded, jnp.float32(0.0))
    totals = jnp.sum(squared, axis=(0, 2), keepdims=True)
    return (TOPK * squared / (totals + 1e-06)).astype(jnp.bfloat16)


def shards(tiles, offsets, counts, ranks):
    panels = tiles.shape[0]
    slots = tiles.shape[1]
    bands = ranks.shape[1]
    total = offsets.shape[0]
    first_panel = lax.axis_index("col") * panels
    pad_off = jnp.concatenate(
        [jnp.zeros((W, slots), jnp.int32), offsets, jnp.zeros((W, slots), jnp.int32)], axis=0
    )
    pad_cnt = jnp.concatenate(
        [jnp.zeros((W,), jnp.int32), counts, jnp.zeros((W,), jnp.int32)], axis=0
    )
    sections = lax.axis_size("section")
    share = panels // sections
    start = first_panel + lax.axis_index("section") * share
    sliced = extended(tiles, (("col", 0),), W)
    windows = jnp.stack([sliced[t * share : t * share + share + 2 * W] for t in range(sections)], 0)
    whole = lax.all_to_all(windows, "section", split_axis=0, concat_axis=3, tiled=True)[0]
    win_off = lax.dynamic_slice_in_dim(pad_off, start, share + 2 * W, 0)
    win_cnt = lax.dynamic_slice_in_dim(pad_cnt, start, share + 2 * W, 0)
    loc_off = lax.dynamic_slice_in_dim(offsets, start, share, 0)
    loc_cnt = lax.dynamic_slice_in_dim(counts, start, share, 0)

    def one_whole(packed):
        p_off, p_cnt, centre = packed
        own = lax.dynamic_index_in_dim(whole, centre + W, 0, False)
        return expand(
            own, p_off, p_cnt, centre, start + centre, whole, win_off, win_cnt, total, bands
        )

    expanded = lax.map(one_whole, (loc_off, loc_cnt, jnp.arange(share, dtype=jnp.int32)))
    back = exchange_in_pieces(expanded, "section", 2, 2, 0)

    def one_finish(packed):
        values, rank_block = packed
        return finish(values, rank_block)

    return lax.map(one_finish, (back, ranks))


def solution(mesh):
    placed = (P("col", None, "section", None), P(), P(), P("col", None, "section", None))
    return jax.shard_map(
        shards,
        mesh=mesh,
        in_specs=placed,
        out_specs=P("col", None, "section", None),
        check_vma=False,
    )
```

profile of v0, /device:TPU:14, one launch (start us, length us, event | category | flops | bytes accessed | tf_op | source)
XLA Modules:
  0.0 642.6 jit_solution(12305052271781320024)
XLA Ops:
  1.3 1.9 collective-permute-start
  3.2 3.6 collective-permute-start.1
  6.9 2.5 collective-permute-done
  19.7 8.6 %all-to-all-start = ((bf16[8,16,12,16,128]{4,3,2,1,0:T(8,128)(2,1)}), bf16[8,16,12,16,128]{4,3,2,1,0:T(8,128)(2,1)}, u32[]{:S(2)}, u32[]{:S(2)}) async-start(bf16[8,16,12,16,128]{4,3,2,1,0:T(8,128)(2,1)} %fusion.11), calls=%async_computation | async-start | bytes 12582912 | tf_op jit(solution)/shard_map/all_to_all | solution.py:94
  29.0 140.1 %all-to-all-done = bf16[8,16,12,16,128]{4,3,2,1,0:T(8,128)(2,1)} async-done(((bf16[8,16,12,16,128]{4,3,2,1,0:T(8,128)(2,1)}), bf16[8,16,12,16,128]{4,3,2,1,0:T(8,128)(2,1)}, u32[]{:S(2)}, u32[]{:S(2)}) %all-to-all-start) | async-done | bytes 6291488 | tf_op jit(solution)/shard_map/all_to_all | solution.py:94
  169.1 7.3 %copy.20 = bf16[1,16,12,8,16,128]{5,4,3,2,1,0:T(8,128)(2,1)} copy(bf16[1,16,12,8,16,128]{5,4,2,1,3,0:T(8,128)(2,1)} %bitcast.21) | data formatting | bytes 12582912 | tf_op jit(solution)/shard_map/all_to_all | solution.py:94
  176.4 199.5 %while.22 = (s32[]{:T(128)}, f32[4,25,128,128]{3,2,1,0:T(8,128)}, s32[4,12]{1,0:T(4,128)S(1)}, s32[4]{0:T(128)S(1)}, s32[16,12]{1,0:T(8,128)S(1)}, /*index=5*/bf...) while((s32[]{:T(128)}, f32[4,25,128,128]{3,2,1,0:T(8,128)}, ...), condition=%wide.region_2.3_spmd, body=%wide.region_0.2_spmd.sunk | while | flops 608701376 | bytes 76102056 | solution.py:107
  181.4 6.3 gather_fusion.2
  187.7 8.0 %broadcast_multiply_fusion.2 = f32[12,12,128,128]{3,2,1,0:T(8,128)} fusion(f32[12,12]{1,0:T(8,128)S(1)} %fusion.27, bf16[12,12,128,128]{3,2,1,0:T(8,128)(2,1)} %gather_fusion.2, bf16[16,12,128,128]{3,2,1,0:T(8,128)(2,1)} %get-tuple-element.310, s32[]{:T(128)S(6)} %select_n.67), kind=kOutput, calls=%fused_computation.10.clone.1 | convolution fusion | flops 606339072 | bytes 14549572 | tf_op jit(solution)/shard_map/while/body/eval_jaxpr/kcx,klxr->klcr/dot_general | solution.py:62
  195.8 9.6 %copy.29 = f32[144,128,128]{2,1,0:T(8,128)} copy(f32[144,128,128]{1,2,0:T(8,128)} %bitcast.73) | data formatting | bytes 18874368 | tf_op jit(solution)/shard_map/while/body/eval_jaxpr/reshape | solution.py:67
  205.8 19.1 %scatter_fusion = f32[25,128,128]{2,1,0:T(8,128)S(1)} fusion(f32[25,128,128]{2,1,0:T(8,128)S(1)} %broadcast.274, s32[144]{0:T(256)S(1)} %bitcast.79, f32[144,128,128]{2,1,0:T(8,128)} %copy.29), kind=kCustom, calls=%fused_computation.3.clone.1 | custom fusion | flops 2359296 | bytes 28312128 | tf_op jit(solution)/shard_map/while/body/eval_jaxpr/scatter-add | solution.py:67
  231.3 6.3 gather_fusion.2
  237.6 8.0 %broadcast_multiply_fusion.2 = f32[12,12,128,128]{3,2,1,0:T(8,128)} fusion(f32[12,12]{1,0:T(8,128)S(1)} %fusion.27, bf16[12,12,128,128]{3,2,1,0:T(8,128)(2,1)} %gather_fusion.2, bf16[16,12,128,128]{3,2,1,0:T(8,128)(2,1)} %get-tuple-element.310, s32[]{:T(128)S(6)} %select_n.67), kind=kOutput, calls=%fused_computation.10.clone.1 | convolution fusion | flops 606339072 | bytes 14549572 | tf_op jit(solution)/shard_map/while/body/eval_jaxpr/kcx,klxr->klcr/dot_general | solution.py:62
  245.6 9.6 %copy.29 = f32[144,128,128]{2,1,0:T(8,128)} copy(f32[144,128,128]{1,2,0:T(8,128)} %bitcast.73) | data formatting | bytes 18874368 | tf_op jit(solution)/shard_map/while/body/eval_jaxpr/reshape | solution.py:67
  255.6 19.1 %scatter_fusion = f32[25,128,128]{2,1,0:T(8,128)S(1)} fusion(f32[25,128,128]{2,1,0:T(8,128)S(1)} %broadcast.274, s32[144]{0:T(256)S(1)} %bitcast.79, f32[144,128,128]{2,1,0:T(8,128)} %copy.29), kind=kCustom, calls=%fused_computation.3.clone.1 | custom fusion | flops 2359296 | bytes 28312128 | tf_op jit(solution)/shard_map/while/body/eval_jaxpr/scatter-add | solution.py:67
  281.1 6.3 gather_fusion.2
  287.4 8.0 %broadcast_multiply_fusion.2 = f32[12,12,128,128]{3,2,1,0:T(8,128)} fusion(f32[12,12]{1,0:T(8,128)S(1)} %fusion.27, bf16[12,12,128,128]{3,2,1,0:T(8,128)(2,1)} %gather_fusion.2, bf16[16,12,128,128]{3,2,1,0:T(8,128)(2,1)} %get-tuple-element.310, s32[]{:T(128)S(6)} %select_n.67), kind=kOutput, calls=%fused_computation.10.clone.1 | convolution fusion | flops 606339072 | bytes 14549572 | tf_op jit(solution)/shard_map/while/body/eval_jaxpr/kcx,klxr->klcr/dot_general | solution.py:62
  295.5 9.6 %copy.29 = f32[144,128,128]{2,1,0:T(8,128)} copy(f32[144,128,128]{1,2,0:T(8,128)} %bitcast.73) | data formatting | bytes 18874368 | tf_op jit(solution)/shard_map/while/body/eval_jaxpr/reshape | solution.py:67
  305.5 19.1 %scatter_fusion = f32[25,128,128]{2,1,0:T(8,128)S(1)} fusion(f32[25,128,128]{2,1,0:T(8,128)S(1)} %broadcast.274, s32[144]{0:T(256)S(1)} %bitcast.79, f32[144,128,128]{2,1,0:T(8,128)} %copy.29), kind=kCustom, calls=%fused_computation.3.clone.1 | custom fusion | flops 2359296 | bytes 28312128 | tf_op jit(solution)/shard_map/while/body/eval_jaxpr/scatter-add | solution.py:67
  330.9 6.3 gather_fusion.2
  337.3 8.0 %broadcast_multiply_fusion.2 = f32[12,12,128,128]{3,2,1,0:T(8,128)} fusion(f32[12,12]{1,0:T(8,128)S(1)} %fusion.27, bf16[12,12,128,128]{3,2,1,0:T(8,128)(2,1)} %gather_fusion.2, bf16[16,12,128,128]{3,2,1,0:T(8,128)(2,1)} %get-tuple-element.310, s32[]{:T(128)S(6)} %select_n.67), kind=kOutput, calls=%fused_computation.10.clone.1 | convolution fusion | flops 606339072 | bytes 14549572 | tf_op jit(solution)/shard_map/while/body/eval_jaxpr/kcx,klxr->klcr/dot_general | solution.py:62
  345.3 9.6 %copy.29 = f32[144,128,128]{2,1,0:T(8,128)} copy(f32[144,128,128]{1,2,0:T(8,128)} %bitcast.73) | data formatting | bytes 18874368 | tf_op jit(solution)/shard_map/while/body/eval_jaxpr/reshape | solution.py:67
  355.3 19.1 %scatter_fusion = f32[25,128,128]{2,1,0:T(8,128)S(1)} fusion(f32[25,128,128]{2,1,0:T(8,128)S(1)} %broadcast.274, s32[144]{0:T(256)S(1)} %bitcast.79, f32[144,128,128]{2,1,0:T(8,128)} %copy.29), kind=kCustom, calls=%fused_computation.3.clone.1 | custom fusion | flops 2359296 | bytes 28312128 | tf_op jit(solution)/shard_map/while/body/eval_jaxpr/scatter-add | solution.py:67
  375.8 3.5 copy.27
  379.3 2.7 copy-done
  383.6 3.6 all-to-all-start.1
  387.2 4.8 split.9
  392.0 46.8 %all-to-all-done.1 = f32[8,4,8,16,128]{4,3,2,1,0:T(8,128)S(1)} async-done(((f32[8,4,8,16,128]{4,3,2,1,0:T(8,128)}), f32[8,4,8,16,128]{4,3,2,1,0:T(8,128)S(1)}, u32[]{:S(2)}, u32[]{:S(2)}) %all-to-all-start.1) | async-done | bytes 2097184 | tf_op jit(solution)/shard_map/all_to_all | solution.py:45
  438.8 4.6 all-to-all-start.2
  443.4 99.3 %all-to-all-done.2 = f32[8,4,17,16,128]{4,3,2,1,0:T(8,128)} async-done(((f32[8,4,17,16,128]{4,3,2,1,0:T(8,128)}), f32[8,4,17,16,128]{4,3,2,1,0:T(8,128)}, u32[]{:S(2)}, u32[]{:S(2)}) %all-to-all-start.2) | async-done | bytes 4456480 | tf_op jit(solution)/shard_map/all_to_all | solution.py:45
  542.7 5.6 pad_maximum_fusion
  548.3 94.4 %while.23 = (s32[]{:T(128)}, bf16[32,25,16,128]{3,2,1,0:T(8,128)(2,1)}, s32[32,25,16,128]{3,2,1,0:T(8,128)}, f32[32,25,16,128]{3,2,1,0:T(8,128)}, s32[]{:T(128)}) while((s32[]{:T(128)}, bf16[32,25,16,128]{3,2,1,0:T(8,128)(2,1)}, s32[32,25,16,128]{3,2,1,0:T(8,128)}, f32[32,25,16,128]{3,2,1,0:T(8,128)}, s32[]{:T(128)}) %tuple.56), condition=%wide.region_5.6_spmd, body=%wide.region_3.5_spmd.sunk | while | flops 512002 | bytes 922433 | solution.py:114
  (186 shorter events, 127.4 us)
Async XLA Ops:
  0.0 13.3 %copy-start.1 = (bf16[32,12,16,128]{3,2,1,0:T(8,128)(2,1)S(1)}, bf16[32,12,16,128]{3,2,1,0:T(8,128)(2,1)}, u32[]{:S(2)}) copy-start(bf16[32,12,16,128]{3,2,1,0:T(8,128)(2,1)} %param.8) | copy-start | bytes 4718596
  1.3 8.0 %collective-permute-start = (bf16[6,12,16,128]{3,2,1,0:T(8,128)(2,1)S(1)}, bf16[6,12,16,128]{3,2,1,0:T(8,128)(2,1)S(1)}, u32[]{:S(2)}, u32[]{:S(2)}) collective-permute-start(bf16[6,12,16,128]{3,2,1,0:T(8,128)(2,1)S(1)} %get-tuple-element.184), channel_id=1, source_target_pairs={{0,1},{1,2},{2,3},{3,4},{4,5},{5,6},{6,7},{7,8},{8,9},{9,10},{10,1... | collective-permute-start | bytes 884744 | tf_op jit(solution)/shard_map/ppermute | solution.py:17
  3.2 14.4 %collective-permute-start.1 = (bf16[6,12,16,128]{3,2,1,0:T(8,128)(2,1)S(1)}, bf16[6,12,16,128]{3,2,1,0:T(8,128)(2,1)S(1)}, u32[]{:S(2)}, u32[]{:S(2)}) collective-permute-start(bf16[6,12,16,128]{3,2,1,0:T(8,128)(2,1)S(1)} %get-tuple-element.183), channel_id=1, source_target_pairs={{1,0},{2,1},{3,2},{4,3},{5,4},{6,5},{7,6},{8,7},{9,8},{10,9},{11,1... | collective-permute-start | bytes 884744 | tf_op jit(solution)/shard_map/ppermute | solution.py:18
  19.7 8.6 %copy-start.2 = (s32[1024,12]{0,1:T(8,128)S(1)}, s32[1024,12]{0,1:T(8,128)}, u32[]{:S(2)}) copy-start(s32[1024,12]{0,1:T(8,128)} %param.9) | copy-start | bytes 147460
  19.7 8.9 %copy-start.3 = (s32[1024]{0:T(1024)S(1)}, s32[1024]{0:T(1024)}, u32[]{:S(2)}) copy-start(s32[1024]{0:T(1024)} %param.10) | copy-start | bytes 12292
  19.7 149.4 %all-to-all-start = ((bf16[8,16,12,16,128]{4,3,2,1,0:T(8,128)(2,1)}), bf16[8,16,12,16,128]{4,3,2,1,0:T(8,128)(2,1)}, u32[]{:S(2)}, u32[]{:S(2)}) async-start(bf16[8,16,12,16,128]{4,3,2,1,0:T(8,128)(2,1)} %fusion.11), calls=%async_computation | async-start | bytes 12582912 | tf_op jit(solution)/shard_map/all_to_all | solution.py:94
  379.3 2.7 copy-start
  383.6 55.2 %all-to-all-start.1 = ((f32[8,4,8,16,128]{4,3,2,1,0:T(8,128)}), f32[8,4,8,16,128]{4,3,2,1,0:T(8,128)S(1)}, u32[]{:S(2)}, u32[]{:S(2)}) async-start(f32[8,4,8,16,128]{4,3,2,1,0:T(8,128)} %split.8), calls=%async_computation.1 | async-start | bytes 4194304 | tf_op jit(solution)/shard_map/all_to_all | solution.py:45
  438.8 103.9 %all-to-all-start.2 = ((f32[8,4,17,16,128]{4,3,2,1,0:T(8,128)}), f32[8,4,17,16,128]{4,3,2,1,0:T(8,128)}, u32[]{:S(2)}, u32[]{:S(2)}) async-start(f32[8,4,17,16,128]{4,3,2,1,0:T(8,128)} %split.9), calls=%async_computation.2 | async-start | bytes 8912896 | tf_op jit(solution)/shard_map/all_to_all | solution.py:45
where the time goes:
time: 647 us; the launch traced here: 643 us
  waiting for transfers between devices  289 us (45%)
  other arithmetic  179 us (28%)
  local copies, waits for them, and re-layouts  112 us (17%)
  matrix products  32.2 us (5%)
  starting transfers between devices  22.4 us (3%)
  loops' own time  8.03 us (1%)
    all_to_all x2, waiting for transfers between devices, exchange_in_pieces(): lax.all_to_all(share, axis, split_axis=0, concat_axis=0, tiled=True)  146 us
    all_to_all x1, waiting for transfers between devices, shards(): lax.all_to_all(windows, 'section', split_axis=0, concat_axis=3, tiled=True)  140 us
    scatter-add x4, other arithmetic, expand(): empty.at[target.reshape(-1)]  76.5 us
    dynamic_update_slice x32, other arithmetic, shards(): return lax.map(one_finish, (back, ranks))  56.6 us
    reshape x4, local copies, waits for them, and re-layouts, expand(): weighted.reshape((slots * slots, columns, rows))  38.3 us
    reduce_sum x32, other arithmetic, finish(): totals = jnp.sum(squared, axis=(0, 2), keepdims=True)  37.5 us
    dot_general x4, matrix products, expand(): jnp.einsum('kcx,klxr->klcr', own, firsts, preferred_element_type=jnp.floa...  32.2 us
    gather x4, local copies, waits for them, and re-layouts, expand(): firsts = banded[where_at]  25.3 us
  transfers between devices with their start and end apart: 5, of which 4 were waited for; matrix products, arithmetic and copies ran while one was open for 2% of the time, Pallas kernels for 0%

commit v1 on v0

--- a/solution.py
+++ b/solution.py
@@ -5,6 +5,22 @@
 
 W = 6
 TOPK = 256
+
+
+def swapped_with_each(x, axis, split, join):
+    ways, here = (lax.axis_size(axis), lax.axis_index(axis))
+    width = x.shape[split] // ways
+    shape = list(x.shape)
+    shape[split] = width
+    height = shape[join]
+    shape[join] = height * ways
+    full = jnp.zeros(shape, x.dtype)
+    for mask in range(ways):
+        part = lax.dynamic_slice_in_dim(x, (here ^ mask) * width, width, axis=split)
+        if mask:
+            part = lax.ppermute(part, axis, [(d, d ^ mask) for d in range(ways)])
+        full = lax.dynamic_update_slice_in_dim(full, part, (here ^ mask) * height, axis=join)
+    return full
 
 
 def extended(shard, sides, width):
@@ -91,7 +107,7 @@
     start = first_panel + lax.axis_index("section") * share
     sliced = extended(tiles, (("col", 0),), W)
     windows = jnp.stack([sliced[t * share : t * share + share + 2 * W] for t in range(sections)], 0)
-    whole = lax.all_to_all(windows, "section", split_axis=0, concat_axis=3, tiled=True)[0]
+    whole = swapped_with_each(windows, "section", 0, 3)[0]
     win_off = lax.dynamic_slice_in_dim(pad_off, start, share + 2 * W, 0)
     win_cnt = lax.dynamic_slice_in_dim(pad_cnt, start, share + 2 * W, 0)
     loc_off = lax.dynamic_slice_in_dim(offsets, start, share, 0)

time: 647 us -> 658 us (1.017)
  starting transfers between devices: 22.4 us -> 50.2 us
  waiting for transfers between devices: 289 us -> 270 us
    all_to_all x1 -> x0, waiting for transfers between devices: 140 us -> none  [shards(): lax.all_to_all(windows, 'section', split_axis=0, concat_axis=3, tiled=True)]
    ppermute x0 -> x7, waiting for transfers between devices: none -> 118 us  [swapped_with_each(): part = lax.ppermute(part, axis, [(d, d ^ mask) for d in range(ways)])]
    ppermute x0 -> x7, starting transfers between devices: none -> 33.1 us  [swapped_with_each(): part = lax.ppermute(part, axis, [(d, d ^ mask) for d in range(ways)])]
    all_to_all x1 -> x0, starting transfers between devices: 8.6 us -> none  [shards(): lax.all_to_all(windows, 'section', split_axis=0, concat_axis=3, tiled=True)]
    all_to_all x1 -> x0, local copies, waits for them, and re-layouts: 7.25 us -> none  [shards(): lax.all_to_all(windows, 'section', split_axis=0, concat_axis=3, tiled=True)]
  transfers between devices with their start and end apart: 5 -> 11, of which waited for: 4 -> 9; matrix products, arithmetic and copies ran while one was open for 2% -> 2% of each run, Pallas kernels for 0% -> 0%
where the time goes in v1:
time: 658 us; the launch traced here: 653 us
  waiting for transfers between devices  270 us (41%)
  other arithmetic  179 us (27%)
  local copies, waits for them, and re-layouts  113 us (17%)
  starting transfers between devices  50.2 us (8%)
  matrix products  32.2 us (5%)
  loops' own time  8.16 us (1%)
    all_to_all x2, waiting for transfers between devices, exchange_in_pieces(): lax.all_to_all(share, axis, split_axis=0, concat_axis=0, tiled=True)  150 us
    ppermute x7, waiting for transfers between devices, swapped_with_each(): part = lax.ppermute(part, axis, [(d, d ^ mask) for d in range(ways)])  118 us
    scatter-add x4, other arithmetic, expand(): empty.at[target.reshape(-1)]  76.5 us
    dynamic_update_slice x32, other arithmetic, shards(): return lax.map(one_finish, (back, ranks))  56.6 us
    reshape x4, local copies, waits for them, and re-layouts, expand(): weighted.reshape((slots * slots, columns, rows))  38.3 us
    reduce_sum x32, other arithmetic, finish(): totals = jnp.sum(squared, axis=(0, 2), keepdims=True)  37.5 us
    ppermute x7, starting transfers between devices, swapped_with_each(): part = lax.ppermute(part, axis, [(d, d ^ mask) for d in range(ways)])  33.1 us
    dot_general x4, matrix products, expand(): jnp.einsum('kcx,klxr->klcr', own, firsts, preferred_element_type=jnp.floa...  32.2 us
  transfers between devices with their start and end apart: 11, of which 9 were waited for; matrix products, arithmetic and copies ran while one was open for 2% of the time, Pallas kernels for 0%

profile of v1, /device:TPU:14, one launch (start us, length us, event | category | flops | bytes accessed | tf_op | source)
XLA Modules:
  0.0 653.3 jit_solution(8443692112354358885)
XLA Ops:
  23.6 6.4 collective-permute-start.5
  33.0 25.3 %collective-permute-done.2 = bf16[1,16,12,16,128]{4,3,2,1,0:T(8,128)(2,1)} collective-permute-done((bf16[1,16,12,16,128]{4,3,2,1,0:T(8,128)(2,1)}, bf16[1,16,12,16,128]{4,3,2,1,0:T(8,128)(2,1)}, u32[]{:S(2)}, u32[]{:S(2)}) %collective-permute-start.2) | collective-permute-done | bytes 786464 | tf_op jit(solution)/shard_map/ppermute | solution.py:21
  58.3 18.6 %collective-permute-start.7 = (bf16[1,16,12,16,128]{4,3,2,1,0:T(8,128)(2,1)S(1)}, bf16[1,16,12,16,128]{4,3,2,1,0:T(8,128)(2,1)S(1)}, u32[]{:S(2)}, u32[]{:S(2)}) collective-permute-start(bf16[1,16,12,16,128]{4,3,2,1,0:T(8,128)(2,1)S(1)} %get-tuple-element.184), channel_id=1, source_target_pairs={{0,192},{32,224},{64,128},{96,160},{128,64},{160,96},{192,0},{224,... | collective-permute-start | bytes 2359304 | tf_op jit(solution)/shard_map/ppermute | solution.py:21
  78.2 11.7 %collective-permute-done.3 = bf16[1,16,12,16,128]{4,3,2,1,0:T(8,128)(2,1)} collective-permute-done((bf16[1,16,12,16,128]{4,3,2,1,0:T(8,128)(2,1)}, bf16[1,16,12,16,128]{4,3,2,1,0:T(8,128)(2,1)}, u32[]{:S(2)}, u32[]{:S(2)}) %collective-permute-start.3) | collective-permute-done | bytes 786464 | tf_op jit(solution)/shard_map/ppermute | solution.py:21
  94.1 45.6 %collective-permute-done.4 = bf16[1,16,12,16,128]{4,3,2,1,0:T(8,128)(2,1)} collective-permute-done((bf16[1,16,12,16,128]{4,3,2,1,0:T(8,128)(2,1)}, bf16[1,16,12,16,128]{4,3,2,1,0:T(8,128)(2,1)}, u32[]{:S(2)}, u32[]{:S(2)}) %collective-permute-start.4) | collective-permute-done | bytes 786464 | tf_op jit(solution)/shard_map/ppermute | solution.py:21
  141.1 16.0 %collective-permute-done.5 = bf16[1,16,12,16,128]{4,3,2,1,0:T(8,128)(2,1)S(1)} collective-permute-done((bf16[1,16,12,16,128]{4,3,2,1,0:T(8,128)(2,1)S(1)}, bf16[1,16,12,16,128]{4,3,2,1,0:T(8,128)(2,1)S(1)}, u32[]{:S(2)}, u32[]{:S(2)}) %collective-permute-start.5) | collective-permute-done | bytes 786464 | tf_op jit(solution)/shard_map/ppermute | solution.py:21
  157.3 5.0 collective-permute-done.6
  162.8 14.5 %collective-permute-done.8 = bf16[1,16,12,16,128]{4,3,2,1,0:T(8,128)(2,1)S(1)} collective-permute-done((bf16[1,16,12,16,128]{4,3,2,1,0:T(8,128)(2,1)S(1)}, bf16[1,16,12,16,128]{4,3,2,1,0:T(8,128)(2,1)S(1)}, u32[]{:S(2)}, u32[]{:S(2)}) %collective-permute-start.8) | collective-permute-done | bytes 786464 | tf_op jit(solution)/shard_map/ppermute | solution.py:21
  180.2 199.6 %while.22 = (s32[]{:T(128)}, f32[4,25,128,128]{3,2,1,0:T(8,128)}, s32[4,12]{1,0:T(4,128)S(1)}, s32[4]{0:T(128)S(1)}, s32[16,12]{1,0:T(8,128)S(1)}, /*index=5*/bf...) while((s32[]{:T(128)}, f32[4,25,128,128]{3,2,1,0:T(8,128)}, ...), condition=%wide.region_2.3_spmd, body=%wide.region_0.2_spmd.sunk | while | flops 608701376 | bytes 76102056 | solution.py:123
  185.2 6.3 gather_fusion.2
  191.6 8.0 %broadcast_multiply_fusion.2 = f32[12,12,128,128]{3,2,1,0:T(8,128)} fusion(f32[12,12]{1,0:T(8,128)S(1)} %fusion.27, bf16[12,12,128,128]{3,2,1,0:T(8,128)(2,1)} %gather_fusion.2, bf16[16,12,128,128]{3,2,1,0:T(8,128)(2,1)} %get-tuple-element.317, s32[]{:T(128)S(6)} %select_n.131), kind=kOutput, calls=%fused_computation.10.clone.1 | convolution fusion | flops 606339072 | bytes 14549572 | tf_op jit(solution)/shard_map/while/body/eval_jaxpr/kcx,klxr->klcr/dot_general | solution.py:78
  199.6 9.6 %copy.26 = f32[144,128,128]{2,1,0:T(8,128)} copy(f32[144,128,128]{1,2,0:T(8,128)} %bitcast.85) | data formatting | bytes 18874368 | tf_op jit(solution)/shard_map/while/body/eval_jaxpr/reshape | solution.py:83
  209.6 19.1 %scatter_fusion = f32[25,128,128]{2,1,0:T(8,128)S(1)} fusion(f32[25,128,128]{2,1,0:T(8,128)S(1)} %broadcast.276, s32[144]{0:T(256)S(1)} %bitcast.90, f32[144,128,128]{2,1,0:T(8,128)} %copy.26), kind=kCustom, calls=%fused_computation.3.clone.1 | custom fusion | flops 2359296 | bytes 28312128 | tf_op jit(solution)/shard_map/while/body/eval_jaxpr/scatter-add | solution.py:83
  235.1 6.3 gather_fusion.2
  241.4 8.0 %broadcast_multiply_fusion.2 = f32[12,12,128,128]{3,2,1,0:T(8,128)} fusion(f32[12,12]{1,0:T(8,128)S(1)} %fusion.27, bf16[12,12,128,128]{3,2,1,0:T(8,128)(2,1)} %gather_fusion.2, bf16[16,12,128,128]{3,2,1,0:T(8,128)(2,1)} %get-tuple-element.317, s32[]{:T(128)S(6)} %select_n.131), kind=kOutput, calls=%fused_computation.10.clone.1 | convolution fusion | flops 606339072 | bytes 14549572 | tf_op jit(solution)/shard_map/while/body/eval_jaxpr/kcx,klxr->klcr/dot_general | solution.py:78
  249.4 9.6 %copy.26 = f32[144,128,128]{2,1,0:T(8,128)} copy(f32[144,128,128]{1,2,0:T(8,128)} %bitcast.85) | data formatting | bytes 18874368 | tf_op jit(solution)/shard_map/while/body/eval_jaxpr/reshape | solution.py:83
  259.5 19.1 %scatter_fusion = f32[25,128,128]{2,1,0:T(8,128)S(1)} fusion(f32[25,128,128]{2,1,0:T(8,128)S(1)} %broadcast.276, s32[144]{0:T(256)S(1)} %bitcast.90, f32[144,128,128]{2,1,0:T(8,128)} %copy.26), kind=kCustom, calls=%fused_computation.3.clone.1 | custom fusion | flops 2359296 | bytes 28312128 | tf_op jit(solution)/shard_map/while/body/eval_jaxpr/scatter-add | solution.py:83
  284.9 6.3 gather_fusion.2
  291.3 8.0 %broadcast_multiply_fusion.2 = f32[12,12,128,128]{3,2,1,0:T(8,128)} fusion(f32[12,12]{1,0:T(8,128)S(1)} %fusion.27, bf16[12,12,128,128]{3,2,1,0:T(8,128)(2,1)} %gather_fusion.2, bf16[16,12,128,128]{3,2,1,0:T(8,128)(2,1)} %get-tuple-element.317, s32[]{:T(128)S(6)} %select_n.131), kind=kOutput, calls=%fused_computation.10.clone.1 | convolution fusion | flops 606339072 | bytes 14549572 | tf_op jit(solution)/shard_map/while/body/eval_jaxpr/kcx,klxr->klcr/dot_general | solution.py:78
  299.3 9.6 %copy.26 = f32[144,128,128]{2,1,0:T(8,128)} copy(f32[144,128,128]{1,2,0:T(8,128)} %bitcast.85) | data formatting | bytes 18874368 | tf_op jit(solution)/shard_map/while/body/eval_jaxpr/reshape | solution.py:83
  309.3 19.1 %scatter_fusion = f32[25,128,128]{2,1,0:T(8,128)S(1)} fusion(f32[25,128,128]{2,1,0:T(8,128)S(1)} %broadcast.276, s32[144]{0:T(256)S(1)} %bitcast.90, f32[144,128,128]{2,1,0:T(8,128)} %copy.26), kind=kCustom, calls=%fused_computation.3.clone.1 | custom fusion | flops 2359296 | bytes 28312128 | tf_op jit(solution)/shard_map/while/body/eval_jaxpr/scatter-add | solution.py:83
  334.8 6.3 gather_fusion.2
  341.2 8.0 %broadcast_multiply_fusion.2 = f32[12,12,128,128]{3,2,1,0:T(8,128)} fusion(f32[12,12]{1,0:T(8,128)S(1)} %fusion.27, bf16[12,12,128,128]{3,2,1,0:T(8,128)(2,1)} %gather_fusion.2, bf16[16,12,128,128]{3,2,1,0:T(8,128)(2,1)} %get-tuple-element.317, s32[]{:T(128)S(6)} %select_n.131), kind=kOutput, calls=%fused_computation.10.clone.1 | convolution fusion | flops 606339072 | bytes 14549572 | tf_op jit(solution)/shard_map/while/body/eval_jaxpr/kcx,klxr->klcr/dot_general | solution.py:78
  349.2 9.6 %copy.26 = f32[144,128,128]{2,1,0:T(8,128)} copy(f32[144,128,128]{1,2,0:T(8,128)} %bitcast.85) | data formatting | bytes 18874368 | tf_op jit(solution)/shard_map/while/body/eval_jaxpr/reshape | solution.py:83
  359.2 19.1 %scatter_fusion = f32[25,128,128]{2,1,0:T(8,128)S(1)} fusion(f32[25,128,128]{2,1,0:T(8,128)S(1)} %broadcast.276, s32[144]{0:T(256)S(1)} %bitcast.90, f32[144,128,128]{2,1,0:T(8,128)} %copy.26), kind=kCustom, calls=%fused_computation.3.clone.1 | custom fusion | flops 2359296 | bytes 28312128 | tf_op jit(solution)/shard_map/while/body/eval_jaxpr/scatter-add | solution.py:83
  387.5 6.9 %all-to-all-start = ((f32[8,4,8,16,128]{4,3,2,1,0:T(8,128)}), f32[8,4,8,16,128]{4,3,2,1,0:T(8,128)S(1)}, u32[]{:S(2)}, u32[]{:S(2)}) async-start(f32[8,4,8,16,128]{4,3,2,1,0:T(8,128)} %split.8), calls=%async_computation | async-start | bytes 4194304 | tf_op jit(solution)/shard_map/all_to_all | solution.py:61
  394.4 4.8 split.9
  399.2 47.2 %all-to-all-done = f32[8,4,8,16,128]{4,3,2,1,0:T(8,128)S(1)} async-done(((f32[8,4,8,16,128]{4,3,2,1,0:T(8,128)}), f32[8,4,8,16,128]{4,3,2,1,0:T(8,128)S(1)}, u32[]{:S(2)}, u32[]{:S(2)}) %all-to-all-start) | async-done | bytes 2097184 | tf_op jit(solution)/shard_map/all_to_all | solution.py:61
  446.4 4.6 all-to-all-start.1
  451.0 102.4 %all-to-all-done.1 = f32[8,4,17,16,128]{4,3,2,1,0:T(8,128)} async-done(((f32[8,4,17,16,128]{4,3,2,1,0:T(8,128)}), f32[8,4,17,16,128]{4,3,2,1,0:T(8,128)}, u32[]{:S(2)}, u32[]{:S(2)}) %all-to-all-start.1) | async-done | bytes 4456480 | tf_op jit(solution)/shard_map/all_to_all | solution.py:61
  553.4 5.6 pad_maximum_fusion
  558.9 94.4 %while.23 = (s32[]{:T(128)}, bf16[32,25,16,128]{3,2,1,0:T(8,128)(2,1)}, s32[32,25,16,128]{3,2,1,0:T(8,128)}, f32[32,25,16,128]{3,2,1,0:T(8,128)}, s32[]{:T(128)}) while((s32[]{:T(128)}, bf16[32,25,16,128]{3,2,1,0:T(8,128)(2,1)}, s32[32,25,16,128]{3,2,1,0:T(8,128)}, f32[32,25,16,128]{3,2,1,0:T(8,128)}, s32[]{:T(128)}) %tuple.62), condition=%wide.region_5.6_spmd, body=%wide.region_3.5_spmd.sunk | while | flops 512002 | bytes 922433 | solution.py:130
  (211 shorter events, 158.2 us)
Async XLA Ops:
  0.0 11.6 %copy-start.2 = (bf16[32,12,16,128]{3,2,1,0:T(8,128)(2,1)S(1)}, bf16[32,12,16,128]{3,2,1,0:T(8,128)(2,1)}, u32[]{:S(2)}) copy-start(bf16[32,12,16,128]{3,2,1,0:T(8,128)(2,1)} %param.8) | copy-start | bytes 4718596
  1.3 8.0 %collective-permute-start = (bf16[6,12,16,128]{3,2,1,0:T(8,128)(2,1)S(1)}, bf16[6,12,16,128]{3,2,1,0:T(8,128)(2,1)S(1)}, u32[]{:S(2)}, u32[]{:S(2)}) collective-permute-start(bf16[6,12,16,128]{3,2,1,0:T(8,128)(2,1)S(1)} %get-tuple-element.191), channel_id=1, source_target_pairs={{0,1},{1,2},{2,3},{3,4},{4,5},{5,6},{6,7},{7,8},{8,9},{9,10},{10,1... | collective-permute-start | bytes 884744 | tf_op jit(solution)/shard_map/ppermute | solution.py:33
  3.2 9.2 %collective-permute-start.1 = (bf16[6,12,16,128]{3,2,1,0:T(8,128)(2,1)S(1)}, bf16[6,12,16,128]{3,2,1,0:T(8,128)(2,1)S(1)}, u32[]{:S(2)}, u32[]{:S(2)}) collective-permute-start(bf16[6,12,16,128]{3,2,1,0:T(8,128)(2,1)S(1)} %get-tuple-element.190), channel_id=1, source_target_pairs={{1,0},{2,1},{3,2},{4,3},{5,4},{6,5},{7,6},{8,7},{9,8},{10,9},{11,1... | collective-permute-start | bytes 884744 | tf_op jit(solution)/shard_map/ppermute | solution.py:34
  12.6 10.2 %copy-start.4 = (s32[1024,12]{0,1:T(8,128)S(1)}, s32[1024,12]{0,1:T(8,128)}, u32[]{:S(2)}) copy-start(s32[1024,12]{0,1:T(8,128)} %param.9) | copy-start | bytes 147460
  12.7 10.6 %copy-start.5 = (s32[1024]{0:T(1024)S(1)}, s32[1024]{0:T(1024)}, u32[]{:S(2)}) copy-start(s32[1024]{0:T(1024)} %param.10) | copy-start | bytes 12292
  12.9 2.7 copy-start.3
  17.7 40.6 %collective-permute-start.2 = (bf16[1,16,12,16,128]{4,3,2,1,0:T(8,128)(2,1)}, bf16[1,16,12,16,128]{4,3,2,1,0:T(8,128)(2,1)}, u32[]{:S(2)}, u32[]{:S(2)}) collective-permute-start(bf16[1,16,12,16,128]{4,3,2,1,0:T(8,128)(2,1)} %get-tuple-element.189), channel_id=1, source_target_pairs={{0,32},{32,0},{64,96},{96,64},{128,160},{160,128},{192,224},{224,1... | collective-permute-start | bytes 2359304 | tf_op jit(solution)/shard_map/ppermute | solution.py:21
  19.6 70.3 %collective-permute-start.3 = (bf16[1,16,12,16,128]{4,3,2,1,0:T(8,128)(2,1)}, bf16[1,16,12,16,128]{4,3,2,1,0:T(8,128)(2,1)}, u32[]{:S(2)}, u32[]{:S(2)}) collective-permute-start(bf16[1,16,12,16,128]{4,3,2,1,0:T(8,128)(2,1)} %get-tuple-element.188), channel_id=1, source_target_pairs={{0,64},{32,96},{64,0},{96,32},{128,192},{160,224},{192,128},{224,1... | collective-permute-start | bytes 2359304 | tf_op jit(solution)/shard_map/ppermute | solution.py:21
  23.0 116.7 %collective-permute-start.4 = (bf16[1,16,12,16,128]{4,3,2,1,0:T(8,128)(2,1)}, bf16[1,16,12,16,128]{4,3,2,1,0:T(8,128)(2,1)}, u32[]{:S(2)}, u32[]{:S(2)}) collective-permute-start(bf16[1,16,12,16,128]{4,3,2,1,0:T(8,128)(2,1)} %get-tuple-element.187), channel_id=1, source_target_pairs={{0,96},{32,64},{64,32},{96,0},{128,224},{160,192},{192,160},{224,1... | collective-permute-start | bytes 2359304 | tf_op jit(solution)/shard_map/ppermute | solution.py:21
  23.6 133.4 %collective-permute-start.5 = (bf16[1,16,12,16,128]{4,3,2,1,0:T(8,128)(2,1)S(1)}, bf16[1,16,12,16,128]{4,3,2,1,0:T(8,128)(2,1)S(1)}, u32[]{:S(2)}, u32[]{:S(2)}) collective-permute-start(bf16[1,16,12,16,128]{4,3,2,1,0:T(8,128)(2,1)S(1)} %get-tuple-element.186), channel_id=1, source_target_pairs={{0,128},{32,160},{64,192},{96,224},{128,0},{160,32},{192,64},{224,... | collective-permute-start | bytes 2359304 | tf_op jit(solution)/shard_map/ppermute | solution.py:21
  30.0 132.3 %collective-permute-start.6 = (bf16[1,16,12,16,128]{4,3,2,1,0:T(8,128)(2,1)S(1)}, bf16[1,16,12,16,128]{4,3,2,1,0:T(8,128)(2,1)S(1)}, u32[]{:S(2)}, u32[]{:S(2)}) collective-permute-start(bf16[1,16,12,16,128]{4,3,2,1,0:T(8,128)(2,1)S(1)} %get-tuple-element.185), channel_id=1, source_target_pairs={{0,160},{32,128},{64,224},{96,192},{128,32},{160,0},{192,96},{224,... | collective-permute-start | bytes 2359304 | tf_op jit(solution)/shard_map/ppermute | solution.py:21
  58.3 104.3 %collective-permute-start.7 = (bf16[1,16,12,16,128]{4,3,2,1,0:T(8,128)(2,1)S(1)}, bf16[1,16,12,16,128]{4,3,2,1,0:T(8,128)(2,1)S(1)}, u32[]{:S(2)}, u32[]{:S(2)}) collective-permute-start(bf16[1,16,12,16,128]{4,3,2,1,0:T(8,128)(2,1)S(1)} %get-tuple-element.184), channel_id=1, source_target_pairs={{0,192},{32,224},{64,128},{96,160},{128,64},{160,96},{192,0},{224,... | collective-permute-start | bytes 2359304 | tf_op jit(solution)/shard_map/ppermute | solution.py:21
  89.9 87.4 %collective-permute-start.8 = (bf16[1,16,12,16,128]{4,3,2,1,0:T(8,128)(2,1)S(1)}, bf16[1,16,12,16,128]{4,3,2,1,0:T(8,128)(2,1)S(1)}, u32[]{:S(2)}, u32[]{:S(2)}) collective-permute-start(bf16[1,16,12,16,128]{4,3,2,1,0:T(8,128)(2,1)S(1)} %get-tuple-element.183), channel_id=1, source_target_pairs={{0,224},{32,192},{64,160},{96,128},{128,96},{160,64},{192,32},{224... | collective-permute-start | bytes 2359304 | tf_op jit(solution)/shard_map/ppermute | solution.py:21
  177.5 2.7 copy-start
  383.2 2.7 copy-start.1
  387.5 58.9 %all-to-all-start = ((f32[8,4,8,16,128]{4,3,2,1,0:T(8,128)}), f32[8,4,8,16,128]{4,3,2,1,0:T(8,128)S(1)}, u32[]{:S(2)}, u32[]{:S(2)}) async-start(f32[8,4,8,16,128]{4,3,2,1,0:T(8,128)} %split.8), calls=%async_computation | async-start | bytes 4194304 | tf_op jit(solution)/shard_map/all_to_all | solution.py:61
  446.4 107.0 %all-to-all-start.1 = ((f32[8,4,17,16,128]{4,3,2,1,0:T(8,128)}), f32[8,4,17,16,128]{4,3,2,1,0:T(8,128)}, u32[]{:S(2)}, u32[]{:S(2)}) async-start(f32[8,4,17,16,128]{4,3,2,1,0:T(8,128)} %split.9), calls=%async_computation.1 | async-start | bytes 8912896 | tf_op jit(solution)/shard_map/all_to_all | solution.py:61
